TPU v7x, 32 devices: a whole 2x2x4 slice. The times are simulated.
32 devices in a mesh: heads: 4 (over y, core), blk: 8 (over z, x).
Axes of the slice: x: 2, y: 2, z: 4, core: 2. Of those that a mesh axis runs over, the one named last changes fastest.
Arguments:
- tokens: bfloat16 [4096, 4096], P(('blk', 'heads')), may hold values from -6 to 6
- w_query: bfloat16 [4096, 2048], P('blk', 'heads'), may hold values from -0.75 to 0.75
- key_value_weight: bfloat16 [4096, 2, 512], P('blk', None, 'heads'), may hold values from -0.75 to 0.75
- w_out: bfloat16 [2048, 4096], P(('heads', 'blk')), may hold values from -0.5 to 0.5
- doc_lengths: int32 [16], replicated, may hold values from 1 to 1024, 4096 in all
Outputs:
- attended: bfloat16 [4096, 4096], P(('blk', 'heads'))
Inputs may be any that keep to these rules, and one draw needn't show every extreme that they name: `doc_lengths`: the 16 lengths sum to 4096; the longest document has exactly 1024 tokens.
All inputs are finite; a program needn't handle non-finite values.
Results may differ from a plain program's by a relative error of at most 0.012.
Values may be sent and summed in bfloat16 or wider, within the bound.
A program may use at most 128 MiB of HBM per device.

v0:
```python
import jax
import jax.numpy as jnp
from jax import lax
from jax.sharding import PartitionSpec as P

HEAD_SIZE = 128
norm_epsilon = 1e-05
rope_base = 500000.0
masked_score = -1e30


def shifted(value, axis, steps):
    count = lax.axis_size(axis)
    first, last = (max(0, -steps), min(count, count - steps))
    return lax.ppermute(value, axis, [(source, source + steps) for source in range(first, last)])


def locate_documents(positions, doc_lengths):
    ends = jnp.cumsum(doc_lengths)
    after = positions[:, None] >= ends[None, :]
    ident = jnp.sum(after.astype(jnp.int32), axis=1)
    starts = jnp.sum(jnp.where(after, doc_lengths[None, :], 0), axis=1)
    return (ident, starts)


def apply_rotation(values, relative_offset):
    half = values.shape[-1] // 2
    freqs = jnp.power(rope_base, -2.0 * jnp.arange(half, dtype=jnp.float32) / values.shape[-1])
    angle = relative_offset.astype(jnp.float32)[:, None] * freqs[None, :]
    cosine = jnp.cos(angle)[:, None, :]
    sine = jnp.sin(angle)[:, None, :]
    first = values[..., :half]
    second = values[..., half:]
    return jnp.concatenate(
        [first * cosine - second * sine, second * cosine + first * sine], axis=-1
    )


def on_device(tokens, w_query, key_value_weight, w_out, doc_lengths):
    blk_index = lax.axis_index("blk")
    reach = lax.axis_size("blk") // 4
    values = tokens.astype(jnp.float32)
    normalized_input = (
        values * lax.rsqrt(jnp.mean(values * values, axis=1, keepdims=True) + norm_epsilon)
    ).astype(jnp.bfloat16)
    block_input = lax.all_gather(normalized_input, "heads", axis=0, tiled=True)
    block_rows = block_input.shape[0]
    query_cols = w_query.shape[1]
    kv_cols = key_value_weight.shape[2]
    pieces = (
        lax.all_gather(w_query, "blk", axis=0, tiled=True),
        lax.all_gather(key_value_weight, "blk", axis=0, tiled=True),
    )
    count = pieces[0].shape[0]
    query_part = jnp.dot(block_input, pieces[0], preferred_element_type=jnp.float32)
    keyval_part = jnp.dot(
        block_input, pieces[1].reshape(count, 2 * kv_cols), preferred_element_type=jnp.float32
    )
    positions = blk_index * block_rows + jnp.arange(block_rows, dtype=jnp.int32)
    ident, starts = locate_documents(positions, doc_lengths)
    relative_offset = positions - starts
    query_heads = query_cols // HEAD_SIZE
    kv_heads = kv_cols // HEAD_SIZE
    head_group = query_heads // kv_heads
    query_rows = apply_rotation(
        query_part.reshape(block_rows, query_heads, HEAD_SIZE), relative_offset
    ).astype(jnp.bfloat16)
    query_rows = query_rows.reshape(block_rows, kv_heads, head_group, HEAD_SIZE)
    rotated_keys = apply_rotation(
        keyval_part[:, :kv_cols].reshape(block_rows, kv_heads, HEAD_SIZE), relative_offset
    ).astype(jnp.bfloat16)
    value_rows = (
        keyval_part[:, kv_cols:].reshape(block_rows, kv_heads, HEAD_SIZE).astype(jnp.bfloat16)
    )
    kv_block = jnp.stack([rotated_keys, value_rows], axis=1)
    scale = HEAD_SIZE ** (-0.5)

    def attend_tile(state, kv_now, distance):
        key_pos = (blk_index - distance) * block_rows + jnp.arange(block_rows, dtype=jnp.int32)
        key_doc, unused_k = locate_documents(key_pos, doc_lengths)
        keep = (
            (key_pos[None, :] >= 0)
            & (key_pos[None, :] <= positions[:, None])
            & (key_doc[None, :] == ident[:, None])
        )
        highest, totals, accum = state
        scores = (
            jnp.einsum(
                "qhgd,khd->hgqk", query_rows, kv_now[:, 0], preferred_element_type=jnp.float32
            )
            * scale
        )
        scores = jnp.where(keep, scores, masked_score)
        new_high = jnp.maximum(highest, jnp.max(scores, axis=-1))
        fading = jnp.exp(highest - new_high)
        probs = jnp.where(keep, jnp.exp(scores - new_high[..., None]), 0.0)
        totals = totals * fading + jnp.sum(probs, axis=-1)
        update = jnp.einsum(
            "hgqk,khd->hgqd",
            probs.astype(jnp.bfloat16),
            kv_now[:, 1],
            preferred_element_type=jnp.float32,
        )
        accum = accum * fading[..., None] + update
        return (new_high, totals, accum)

    initial = (
        jnp.full((kv_heads, head_group, block_rows), masked_score, jnp.float32),
        jnp.zeros((kv_heads, head_group, block_rows), jnp.float32),
        jnp.zeros((kv_heads, head_group, block_rows, HEAD_SIZE), jnp.float32),
    )
    state = attend_tile(initial, kv_block, 0)

    def advance(distance, carry):
        kv_now, inner = carry
        kv_now = shifted(kv_now, "blk", 1)
        return (kv_now, attend_tile(inner, kv_now, distance))

    unused_kv, state = lax.fori_loop(1, reach + 1, advance, (kv_block, state))
    highest, totals, accum = state
    mixed = accum / totals[..., None]
    mixed = mixed.transpose(2, 0, 1, 3).reshape(block_rows, query_cols).astype(jnp.bfloat16)
    head_rows = lax.all_gather(w_out, "blk", axis=0, tiled=True)
    return lax.psum_scatter(
        jnp.dot(mixed, head_rows, preferred_element_type=jnp.float32).astype(jnp.bfloat16),
        "heads",
        scatter_dimension=0,
        tiled=True,
    )


def solution(mesh):
    return jax.shard_map(
        on_device,
        mesh=mesh,
        in_specs=(
            P(("blk", "heads"), None),
            P("blk", "heads"),
            P("blk", None, "heads"),
            P(("heads", "blk"), None),
            P(),
        ),
        out_specs=P(("blk", "heads"), None),
        check_vma=False,
    )
```

profile of v0, /device:TPU:0, one launch (start us, length us, event | category | flops | bytes accessed | tf_op | source)
XLA Modules:
  0.0 311.8 jit_solution(1493680241664175790)
XLA Ops:
  7.3 1.5 fusion.24
  8.8 2.5 fusion.25
  13.0 1.0 multiply_cosine_fusion
  14.4 46.9 %all-gather.7.cloned.1.call-done = bf16[4096,2,128]{2,1,0:T(2,128)(2,1)} async-done(((bf16[512,2,128]{2,1,0:T(2,128)(2,1)}), bf16[4096,2,128]{2,1,0:T(2,128)(2,1)}) %all-gather.7.cloned.1.call-update) | async-done | bytes 2097168 | tf_op jit(solution)/shard_map/all_gather | solution.py:52
  61.3 34.6 %all-gather.5.cloned.1.call-done = bf16[512,4096]{1,0:T(8,128)(2,1)} async-done(((bf16[128,4096]{1,0:T(8,128)(2,1)}), bf16[512,4096]{1,0:T(8,128)(2,1)}) %all-gather.5.cloned.1.call-update) | async-done | bytes 4194320 | tf_op jit(solution)/shard_map/all_gather | solution.py:46
  95.9 4.2 %fusion.27 = f32[512,256]{0,1:T(8,128)S(1)} fusion(bf16[512,4096]{1,0:T(8,128)(2,1)} %all-gather.5.cloned.1.call-done, bf16[512,8,2,128]{3,2,1,0:T(2,128)(2,1)} %bitcast.161), kind=kOutput, calls=%fused_computation.38 | convolution fusion | flops 1073741824 | bytes 6815744 | tf_op jit(solution)/shard_map/dot_general | solution.py:56
  101.7 69.1 %all-gather.9.cloned.1.call-done = bf16[4096,512]{1,0:T(8,128)(2,1)} async-done(((bf16[512,512]{1,0:T(8,128)(2,1)}), bf16[4096,512]{1,0:T(8,128)(2,1)}) %all-gather.9.cloned.1.call-update) | async-done | bytes 4194320 | tf_op jit(solution)/shard_map/all_gather | solution.py:51
  170.8 5.8 %fusion.64 = f32[512,512]{0,1:T(8,128)S(1)} fusion(bf16[512,4096]{1,0:T(8,128)(2,1)} %all-gather.5.cloned.1.call-done, bf16[4096,512]{1,0:T(8,128)(2,1)} %all-gather.9.cloned.1.call-done), kind=kOutput, calls=%fused_computation.92 | convolution fusion | flops 2147483648 | bytes 9437184 | tf_op jit(solution)/shard_map/dot_general | solution.py:55
  178.1 1.2 fusion.21
  179.3 1.0 fusion.23
  180.4 1.6 fusion.36
  182.0 29.8 %while.22 = (s32[]{:T(128)}, bf16[512,2,1,128]{3,0,2,1:T(8,128)(2,1)S(1)}, f32[1,4,512]{2,1,0:T(4,128)S(1)}, f32[1,4,512]{2,1,0:T(4,128)S(1)}, f32[1,4,512,128]{...) while((s32[]{:T(128)}, ...), condition=%wide.region_10.11_spmd.clone, body=%wide.region_6.10_spmd.clone.sunk | while | flops 552107520 | bytes 18236672 | solution.py:119
  182.2 2.5 collective-permute-start
  185.1 6.1 %collective-permute-done = bf16[512,2,1,128]{3,0,2,1:T(8,128)(2,1)S(1)} collective-permute-done((bf16[512,2,1,128]{3,0,2,1:T(8,128)(2,1)S(1)}, bf16[512,2,1,128]{3,0,2,1:T(8,128)(2,1)S(1)}, u32[]{:S(2)}, u32[]{:S(2)}) %collective-permute-start) | collective-permute-done | bytes 262176 | tf_op jit(solution)/shard_map/while/body/eval_jaxpr/ppermute | solution.py:15
  192.1 1.0 fusion.78
  193.2 1.9 fusion.79
  195.2 8.8 %collective-permute-start = (bf16[512,2,1,128]{3,0,2,1:T(8,128)(2,1)S(1)}, bf16[512,2,1,128]{3,0,2,1:T(8,128)(2,1)S(1)}, u32[]{:S(2)}, u32[]{:S(2)}) collective-permute-start(bf16[512,2,1,128]{3,0,2,1:T(8,128)(2,1)S(1)} %get-tuple-element.431), channel_id=1, source_target_pairs={{0,1},{1,2},{2,3},{3,4},{4,5},{5,6},{6,7},{8,9},{9,10},{10,11},{11... | collective-permute-start | bytes 786440 | tf_op jit(solution)/shard_map/while/body/eval_jaxpr/ppermute | solution.py:15
  204.4 3.4 %collective-permute-done = bf16[512,2,1,128]{3,0,2,1:T(8,128)(2,1)S(1)} collective-permute-done((bf16[512,2,1,128]{3,0,2,1:T(8,128)(2,1)S(1)}, bf16[512,2,1,128]{3,0,2,1:T(8,128)(2,1)S(1)}, u32[]{:S(2)}, u32[]{:S(2)}) %collective-permute-start) | collective-permute-done | bytes 262176 | tf_op jit(solution)/shard_map/while/body/eval_jaxpr/ppermute | solution.py:15
  207.8 0.9 fusion.76
  208.7 1.0 fusion.78
  209.8 1.9 fusion.79
  212.2 41.3 %all-gather.11.cloned.1.call-done = bf16[512,4096]{1,0:T(8,128)(2,1)} async-done(((bf16[64,4096]{1,0:T(8,128)(2,1)}), bf16[512,4096]{1,0:T(8,128)(2,1)}) %all-gather.11.cloned.1.call-update) | async-done | bytes 4194320 | tf_op jit(solution)/shard_map/all_gather | solution.py:123
  253.6 6.5 %convolution_convert_fusion = bf16[512,4096]{1,0:T(8,128)(2,1)} fusion(bf16[512,512]{0,1:T(8,128)(2,1)S(1)} %bitcast.151, bf16[512,4096]{1,0:T(8,128)(2,1)} %all-gather.11.cloned.1.call-done), kind=kOutput, calls=%fused_computation.27 | convolution fusion | flops 2149580800 | bytes 8912896 | tf_op jit(solution)/shard_map/dot_general | solution.py:125
  260.1 45.2 %reduce-scatter.2.cloned.1.call-done = bf16[128,4096]{1,0:T(8,128)(2,1)} async-done(((bf16[512,4096]{1,0:T(8,128)(2,1)}), bf16[128,4096]{1,0:T(8,128)(2,1)}) %reduce-scatter.2.cloned.1.call-update) | async-done | bytes 1048592 | tf_op jit(solution)/shard_map/reduce_scatter | solution.py:124
  (57 shorter events, 8.1 us)
Async XLA Ops:
  6.5 6.2 %copy-start.3 = (s32[16]{0:T(128)S(1)}, s32[16]{0:T(128)}, u32[]{:S(2)}) copy-start(s32[16]{0:T(128)} %param.11) | copy-start | bytes 196
  6.5 54.8 %all-gather.7.cloned.1.call-start = ((), (), s32[]{:S(2)}) async-start(), calls=%async_computation.2 | async-start | bytes 2359296 | tf_op jit(solution)/shard_map/all_gather | solution.py:52
  7.3 88.6 %all-gather.5.cloned.1.call-start = ((), (), s32[]{:S(2)}) async-start(), calls=%async_computation.1 | async-start | bytes 5242880 | tf_op jit(solution)/shard_map/all_gather | solution.py:46
  11.3 159.5 %all-gather.9.cloned.1.call-start = ((), (), s32[]{:S(2)}) async-start(), calls=%async_computation.3 | async-start | bytes 4718592 | tf_op jit(solution)/shard_map/all_gather | solution.py:51
  12.1 241.5 %all-gather.11.cloned.1.call-start = ((), (), s32[]{:S(2)}) async-start(), calls=%async_computation.4 | async-start | bytes 4718592 | tf_op jit(solution)/shard_map/all_gather | solution.py:123
  12.6 292.7 %reduce-scatter.2.cloned.1.call-start = ((), (), s32[]{:S(2)}) async-start(), calls=%async_computation.5 | async-start | bytes 5242880 | tf_op jit(solution)/shard_map/reduce_scatter | solution.py:124
  100.0 0.8 copy-start
  178.1 2.3 copy-start.1
  180.4 1.6 copy-start.2
  182.2 9.1 %collective-permute-start = (bf16[512,2,1,128]{3,0,2,1:T(8,128)(2,1)S(1)}, bf16[512,2,1,128]{3,0,2,1:T(8,128)(2,1)S(1)}, u32[]{:S(2)}, u32[]{:S(2)}) collective-permute-start(bf16[512,2,1,128]{3,0,2,1:T(8,128)(2,1)S(1)} %get-tuple-element.431), channel_id=1, source_target_pairs={{0,1},{1,2},{2,3},{3,4},{4,5},{5,6},{6,7},{8,9},{9,10},{10,11},{11... | collective-permute-start | bytes 786440 | tf_op jit(solution)/shard_map/while/body/eval_jaxpr/ppermute | solution.py:15
  195.2 12.7 %collective-permute-start = (bf16[512,2,1,128]{3,0,2,1:T(8,128)(2,1)S(1)}, bf16[512,2,1,128]{3,0,2,1:T(8,128)(2,1)S(1)}, u32[]{:S(2)}, u32[]{:S(2)}) collective-permute-start(bf16[512,2,1,128]{3,0,2,1:T(8,128)(2,1)S(1)} %get-tuple-element.431), channel_id=1, source_target_pairs={{0,1},{1,2},{2,3},{3,4},{4,5},{5,6},{6,7},{8,9},{9,10},{10,11},{11... | collective-permute-start | bytes 786440 | tf_op jit(solution)/shard_map/while/body/eval_jaxpr/ppermute | solution.py:15
Sparse Core Ops, SparseCore 0:
  9.5 51.7 all-gather.6
  62.9 32.9 all-gather.4
  98.0 72.7 all-gather.8
  172.8 80.7 all-gather.10
  260.2 45.0 reduce-scatter.1
where the time goes:
time: 312 us
  waiting for transfers between devices  249 us (80%)
  matrix products  24.9 us (8%)
  between operations  13.3 us (4%)
  starting transfers between devices  11.4 us (4%)
  other arithmetic  11 us (4%)
    all_gather x1, waiting for transfers between devices, on_device(): lax.all_gather(w_query, 'blk', axis=0, tiled=True)  69.1 us
    all_gather x1, waiting for transfers between devices, on_device(): lax.all_gather(key_value_weight, 'blk', axis=0, tiled=True)  46.9 us
    reduce_scatter x1, waiting for transfers between devices, on_device(): lax.psum_scatter(jnp.dot(mixed, head_rows, preferred_element_type=jnp.flo...  45.2 us
    all_gather x1, waiting for transfers between devices, on_device(): head_rows = lax.all_gather(w_out, 'blk', axis=0, tiled=True)  41.3 us
    all_gather x1, waiting for transfers between devices, on_device(): block_input = lax.all_gather(normalized_input, 'heads', axis=0, tiled=True)  34.6 us
    ppermute x2, starting transfers between devices, shifted(): lax.ppermute(value, axis, [(source, source + steps) for source in range(f...  11.3 us
    ppermute x2, waiting for transfers between devices, shifted(): lax.ppermute(value, axis, [(source, source + steps) for source in range(f...  9.5 us
    dot_general x1, matrix products, on_device(): jnp.dot(mixed, head_rows, preferred_element_type=jnp.float32)  6.52 us
  transfers between devices with their start and end apart: 7, of which 7 were waited for; matrix products, arithmetic and copies ran while one was open for 10% of the time, Pallas kernels for 0%

commit v1 on v0

--- a/solution.py
+++ b/solution.py
@@ -120,7 +120,12 @@
     highest, totals, accum = state
     mixed = accum / totals[..., None]
     mixed = mixed.transpose(2, 0, 1, 3).reshape(block_rows, query_cols).astype(jnp.bfloat16)
-    head_rows = lax.all_gather(w_out, "blk", axis=0, tiled=True)
+    ring = [w_out]
+    for hop in range(7):
+        ring.append(lax.ppermute(ring[-1], "blk", [(dev, (dev + 1) % 8) for dev in range(8)]))
+    head_rows = jnp.roll(
+        jnp.concatenate(ring[::-1], axis=0), (lax.axis_index("blk") + 1) * ring[0].shape[0], axis=0
+    )
     return lax.psum_scatter(
         jnp.dot(mixed, head_rows, preferred_element_type=jnp.float32).astype(jnp.bfloat16),
         "heads",

time: 312 us -> 294 us (0.942)
  waiting for transfers between devices: 249 us -> 213 us
  local copies, waits for them, and re-layouts: 2.21 us -> 19.9 us
    ppermute x0 -> x7, waiting for transfers between devices: none -> 112 us  [on_device(): lax.ppermute(ring[-1], 'blk', [(dev, (dev + 1) % 8) for dev in range(8)])]
    all_gather x1, waiting for transfers between devices: 46.9 us -> 0.01 us  [on_device(): lax.all_gather(key_value_weight, 'blk', axis=0, tiled=True)]
    all_gather x1 -> x0, waiting for transfers between devices: 41.3 us -> none  [on_device(): head_rows = lax.all_gather(w_out, 'blk', axis=0, tiled=True)]
    all_gather x1, waiting for transfers between devices: 34.6 us -> 0.01 us  [on_device(): block_input = lax.all_gather(normalized_input, 'heads', axis=0, tiled=True)]
    all_gather x1, waiting for transfers between devices: 69.1 us -> 43.4 us  [on_device(): lax.all_gather(w_query, 'blk', axis=0, tiled=True)]
    unnamed x11 -> x32, local copies, waits for them, and re-layouts: 1.69 us -> 18.5 us
    ppermute x2, starting transfers between devices: 11.3 us -> 6.88 us  [shifted(): lax.ppermute(value, axis, [(source, source + steps) for source in range(f...]
    reduce_scatter x1, waiting for transfers between devices: 45.2 us -> 48.8 us  [on_device(): lax.psum_scatter(jnp.dot(mixed, head_rows, preferred_element_type=jnp.flo...]
  transfers between devices with their start and end apart: 7 -> 13, of which waited for: 7 -> 11; matrix products, arithmetic and copies ran while one was open for 10% -> 10% of each run, Pallas kernels for 0% -> 0%
where the time goes in v1:
time: 294 us; the launch traced here: 293 us
  waiting for transfers between devices  213 us (72%)
  matrix products  24.9 us (8%)
  local copies, waits for them, and re-layouts  19.9 us (7%)
  between operations  13.4 us (5%)
  other arithmetic  11.9 us (4%)
  starting transfers between devices  10 us (3%)
    ppermute x7, waiting for transfers between devices, on_device(): lax.ppermute(ring[-1], 'blk', [(dev, (dev + 1) % 8) for dev in range(8)])  112 us
    reduce_scatter x1, waiting for transfers between devices, on_device(): lax.psum_scatter(jnp.dot(mixed, head_rows, preferred_element_type=jnp.flo...  48.8 us
    all_gather x1, waiting for transfers between devices, on_device(): lax.all_gather(w_query, 'blk', axis=0, tiled=True)  43.4 us
    unnamed x32, local copies, waits for them, and re-layouts  18.5 us
    ppermute x2, waiting for transfers between devices, shifted(): lax.ppermute(value, axis, [(source, source + steps) for source in range(f...  7.25 us
    ppermute x2, starting transfers between devices, shifted(): lax.ppermute(value, axis, [(source, source + steps) for source in range(f...  6.88 us
    dot_general x1, matrix products, on_device(): jnp.dot(mixed, head_rows, preferred_element_type=jnp.float32)  6.54 us
  transfers between devices with their start and end apart: 13, of which 11 were waited for; matrix products, arithmetic and copies ran while one was open for 10% of the time, Pallas kernels for 0%

profile of v1, /device:TPU:0, one launch (start us, length us, event | category | flops | bytes accessed | tf_op | source)
XLA Modules:
  0.0 293.2 jit_solution(9226203539502205790)
XLA Ops:
  8.8 2.5 fusion.26
  11.4 3.0 %collective-permute-start.1 = (bf16[64,4096]{1,0:T(8,128)(2,1)S(1)}, bf16[64,4096]{1,0:T(8,128)(2,1)S(1)}, u32[]{:S(2)}, u32[]{:S(2)}) collective-permute-start(bf16[64,4096]{1,0:T(8,128)(2,1)S(1)} %copy-done), channel_id=1, source_target_pairs={{0,1},{1,2},{2,3},{3,4},{4,5},{5,6},{6,7},{7,0},{8,9},{9,10},{10,1... | collective-permute-start | bytes 1572872 | tf_op jit(solution)/shard_map/ppermute | solution.py:125
  14.4 19.4 %collective-permute-done.1 = bf16[64,4096]{1,0:T(8,128)(2,1)S(1)} collective-permute-done((bf16[64,4096]{1,0:T(8,128)(2,1)S(1)}, bf16[64,4096]{1,0:T(8,128)(2,1)S(1)}, u32[]{:S(2)}, u32[]{:S(2)}) %collective-permute-start.1) | collective-permute-done | bytes 524320 | tf_op jit(solution)/shard_map/ppermute | solution.py:125
  33.8 15.3 %collective-permute-done.2 = bf16[64,4096]{1,0:T(8,128)(2,1)S(1)} collective-permute-done((bf16[64,4096]{1,0:T(8,128)(2,1)S(1)}, bf16[64,4096]{1,0:T(8,128)(2,1)S(1)}, u32[]{:S(2)}, u32[]{:S(2)}) %collective-permute-start.2) | collective-permute-done | bytes 524320 | tf_op jit(solution)/shard_map/ppermute | solution.py:125
  49.0 25.4 %collective-permute-done.3 = bf16[64,4096]{1,0:T(8,128)(2,1)S(1)} collective-permute-done((bf16[64,4096]{1,0:T(8,128)(2,1)S(1)}, bf16[64,4096]{1,0:T(8,128)(2,1)S(1)}, u32[]{:S(2)}, u32[]{:S(2)}) %collective-permute-start.3) | collective-permute-done | bytes 524320 | tf_op jit(solution)/shard_map/ppermute | solution.py:125
  74.4 17.2 %collective-permute-done.4 = bf16[64,4096]{1,0:T(8,128)(2,1)S(1)} collective-permute-done((bf16[64,4096]{1,0:T(8,128)(2,1)S(1)}, bf16[64,4096]{1,0:T(8,128)(2,1)S(1)}, u32[]{:S(2)}, u32[]{:S(2)}) %collective-permute-start.4) | collective-permute-done | bytes 524320 | tf_op jit(solution)/shard_map/ppermute | solution.py:125
  91.9 12.9 %collective-permute-done.5 = bf16[64,4096]{1,0:T(8,128)(2,1)S(1)} collective-permute-done((bf16[64,4096]{1,0:T(8,128)(2,1)S(1)}, bf16[64,4096]{1,0:T(8,128)(2,1)S(1)}, u32[]{:S(2)}, u32[]{:S(2)}) %collective-permute-start.5) | collective-permute-done | bytes 524320 | tf_op jit(solution)/shard_map/ppermute | solution.py:125
  105.0 12.4 %collective-permute-done.6 = bf16[64,4096]{1,0:T(8,128)(2,1)} collective-permute-done((bf16[64,4096]{1,0:T(8,128)(2,1)S(1)}, bf16[64,4096]{1,0:T(8,128)(2,1)}, u32[]{:S(2)}, u32[]{:S(2)}) %collective-permute-start.6) | collective-permute-done | bytes 524320 | tf_op jit(solution)/shard_map/ppermute | solution.py:125
  119.5 10.0 %collective-permute-done.7 = bf16[64,4096]{1,0:T(8,128)(2,1)} collective-permute-done((bf16[64,4096]{1,0:T(8,128)(2,1)}, bf16[64,4096]{1,0:T(8,128)(2,1)}, u32[]{:S(2)}, u32[]{:S(2)}) %collective-permute-start.7) | collective-permute-done | bytes 524320 | tf_op jit(solution)/shard_map/ppermute | solution.py:125
  129.5 1.9 constant_dynamic-update-slice_fusion.15
  131.4 1.9 constant_dynamic-update-slice_fusion.14
  138.3 1.9 constant_dynamic-update-slice_fusion.7
  147.2 4.2 %fusion.28 = f32[512,256]{0,1:T(8,128)S(1)} fusion(bf16[512,4096]{1,0:T(8,128)(2,1)} %all-gather.4.cloned.1.call-done, bf16[512,8,2,128]{3,2,1,0:T(2,128)(2,1)} %bitcast.160), kind=kOutput, calls=%fused_computation.39 | convolution fusion | flops 1073741824 | bytes 6815744 | tf_op jit(solution)/shard_map/dot_general | solution.py:56
  152.8 43.4 %all-gather.8.cloned.1.call-done = bf16[4096,512]{1,0:T(8,128)(2,1)} async-done(((bf16[512,512]{1,0:T(8,128)(2,1)}), bf16[4096,512]{1,0:T(8,128)(2,1)}) %all-gather.8.cloned.1.call-update) | async-done | bytes 4194320 | tf_op jit(solution)/shard_map/all_gather | solution.py:51
  196.3 5.8 %fusion.66 = f32[512,512]{0,1:T(8,128)S(1)} fusion(bf16[512,4096]{1,0:T(8,128)(2,1)} %all-gather.4.cloned.1.call-done, bf16[4096,512]{1,0:T(8,128)(2,1)} %all-gather.8.cloned.1.call-done), kind=kOutput, calls=%fused_computation.110 | convolution fusion | flops 2147483648 | bytes 9437184 | tf_op jit(solution)/shard_map/dot_general | solution.py:55
  207.7 23.1 %while.22 = (s32[]{:T(128)}, bf16[512,2,1,128]{3,0,2,1:T(8,128)(2,1)S(1)}, f32[1,4,512]{2,1,0:T(4,128)S(1)}, f32[1,4,512]{2,1,0:T(4,128)S(1)}, f32[1,4,512,128]{...) while((s32[]{:T(128)}, ...), condition=%wide.region_10.11_spmd.clone, body=%wide.region_6.10_spmd.clone.sunk | while | flops 552107520 | bytes 18236672 | solution.py:119
  207.9 2.5 collective-permute-start
  210.8 3.9 %collective-permute-done = bf16[512,2,1,128]{3,0,2,1:T(8,128)(2,1)S(1)} collective-permute-done((bf16[512,2,1,128]{3,0,2,1:T(8,128)(2,1)S(1)}, bf16[512,2,1,128]{3,0,2,1:T(8,128)(2,1)S(1)}, u32[]{:S(2)}, u32[]{:S(2)}) %collective-permute-start) | collective-permute-done | bytes 262176 | tf_op jit(solution)/shard_map/while/body/eval_jaxpr/ppermute | solution.py:15
  216.7 1.9 fusion.80
  218.6 4.4 %collective-permute-start = (bf16[512,2,1,128]{3,0,2,1:T(8,128)(2,1)S(1)}, bf16[512,2,1,128]{3,0,2,1:T(8,128)(2,1)S(1)}, u32[]{:S(2)}, u32[]{:S(2)}) collective-permute-start(bf16[512,2,1,128]{3,0,2,1:T(8,128)(2,1)S(1)} %get-tuple-element.431), channel_id=1, source_target_pairs={{0,1},{1,2},{2,3},{3,4},{4,5},{5,6},{6,7},{8,9},{9,10},{10,11},{11... | collective-permute-start | bytes 786440 | tf_op jit(solution)/shard_map/while/body/eval_jaxpr/ppermute | solution.py:15
  223.5 3.4 %collective-permute-done = bf16[512,2,1,128]{3,0,2,1:T(8,128)(2,1)S(1)} collective-permute-done((bf16[512,2,1,128]{3,0,2,1:T(8,128)(2,1)S(1)}, bf16[512,2,1,128]{3,0,2,1:T(8,128)(2,1)S(1)}, u32[]{:S(2)}, u32[]{:S(2)}) %collective-permute-start) | collective-permute-done | bytes 262176 | tf_op jit(solution)/shard_map/while/body/eval_jaxpr/ppermute | solution.py:15
  228.9 1.9 fusion.80
  231.3 6.5 %convolution_convert_fusion = bf16[512,4096]{1,0:T(8,128)(2,1)} fusion(bf16[512,512]{0,1:T(8,128)(2,1)S(1)} %bitcast.155, bf16[1024,4096]{1,0:T(8,128)(2,1)} %constant_dynamic-update-slice_fusion, s32[]{:T(128)S(6)} %select_n.46), kind=kOutput, calls=%fused_computation.27 | convolution fusion | flops 2149580800 | bytes 8912900 | tf_op jit(solution)/shard_map/dot_general | solution.py:130
  237.9 48.8 %reduce-scatter.2.cloned.1.call-done = bf16[128,4096]{1,0:T(8,128)(2,1)} async-done(((bf16[512,4096]{1,0:T(8,128)(2,1)}), bf16[128,4096]{1,0:T(8,128)(2,1)}) %reduce-scatter.2.cloned.1.call-update) | async-done | bytes 1048592 | tf_op jit(solution)/shard_map/reduce_scatter | solution.py:129
  (90 shorter events, 29.1 us)
Async XLA Ops:
  6.5 4.8 %copy-start = (bf16[64,4096]{1,0:T(8,128)(2,1)S(1)}, bf16[64,4096]{1,0:T(8,128)(2,1)}, u32[]{:S(2)}) copy-start(bf16[64,4096]{1,0:T(8,128)(2,1)} %param.10) | copy-start | bytes 1572868
  6.5 85.2 %copy-start.6 = (s32[16]{0:T(128)S(1)}, s32[16]{0:T(128)}, u32[]{:S(2)}) copy-start(s32[16]{0:T(128)} %param.11) | copy-start | bytes 196
  6.5 140.6 %all-gather.6.cloned.1.call-start = ((), (), s32[]{:S(2)}) async-start(), calls=%async_computation.2 | async-start | bytes 2359296 | tf_op jit(solution)/shard_map/all_gather | solution.py:52
  7.3 139.9 %all-gather.4.cloned.1.call-start = ((), (), s32[]{:S(2)}) async-start(), calls=%async_computation.1 | async-start | bytes 5242880 | tf_op jit(solution)/shard_map/all_gather | solution.py:46
  11.3 185.0 %all-gather.8.cloned.1.call-start = ((), (), s32[]{:S(2)}) async-start(), calls=%async_computation.3 | async-start | bytes 4718592 | tf_op jit(solution)/shard_map/all_gather | solution.py:51
  11.4 22.4 %collective-permute-start.1 = (bf16[64,4096]{1,0:T(8,128)(2,1)S(1)}, bf16[64,4096]{1,0:T(8,128)(2,1)S(1)}, u32[]{:S(2)}, u32[]{:S(2)}) collective-permute-start(bf16[64,4096]{1,0:T(8,128)(2,1)S(1)} %copy-done), channel_id=1, source_target_pairs={{0,1},{1,2},{2,3},{3,4},{4,5},{5,6},{6,7},{7,0},{8,9},{9,10},{10,1... | collective-permute-start | bytes 1572872 | tf_op jit(solution)/shard_map/ppermute | solution.py:125
  33.8 15.3 %collective-permute-start.2 = (bf16[64,4096]{1,0:T(8,128)(2,1)S(1)}, bf16[64,4096]{1,0:T(8,128)(2,1)S(1)}, u32[]{:S(2)}, u32[]{:S(2)}) collective-permute-start(bf16[64,4096]{1,0:T(8,128)(2,1)S(1)} %collective-permute-done.1), channel_id=1, source_target_pairs={{0,1},{1,2},{2,3},{3,4},{4,5},{5,6},{6,7},{7,0},{8,9},{9,10},{10,1... | collective-permute-start | bytes 1572872 | tf_op jit(solution)/shard_map/ppermute | solution.py:125
  49.0 25.4 %collective-permute-start.3 = (bf16[64,4096]{1,0:T(8,128)(2,1)S(1)}, bf16[64,4096]{1,0:T(8,128)(2,1)S(1)}, u32[]{:S(2)}, u32[]{:S(2)}) collective-permute-start(bf16[64,4096]{1,0:T(8,128)(2,1)S(1)} %collective-permute-done.2), channel_id=1, source_target_pairs={{0,1},{1,2},{2,3},{3,4},{4,5},{5,6},{6,7},{7,0},{8,9},{9,10},{10,1... | collective-permute-start | bytes 1572872 | tf_op jit(solution)/shard_map/ppermute | solution.py:125
  74.4 17.2 %collective-permute-start.4 = (bf16[64,4096]{1,0:T(8,128)(2,1)S(1)}, bf16[64,4096]{1,0:T(8,128)(2,1)S(1)}, u32[]{:S(2)}, u32[]{:S(2)}) collective-permute-start(bf16[64,4096]{1,0:T(8,128)(2,1)S(1)} %collective-permute-done.3), channel_id=1, source_target_pairs={{0,1},{1,2},{2,3},{3,4},{4,5},{5,6},{6,7},{7,0},{8,9},{9,10},{10,1... | collective-permute-start | bytes 1572872 | tf_op jit(solution)/shard_map/ppermute | solution.py:125
  91.6 13.2 %collective-permute-start.5 = (bf16[64,4096]{1,0:T(8,128)(2,1)S(1)}, bf16[64,4096]{1,0:T(8,128)(2,1)S(1)}, u32[]{:S(2)}, u32[]{:S(2)}) collective-permute-start(bf16[64,4096]{1,0:T(8,128)(2,1)S(1)} %collective-permute-done.4), channel_id=1, source_target_pairs={{0,1},{1,2},{2,3},{3,4},{4,5},{5,6},{6,7},{7,0},{8,9},{9,10},{10,1... | collective-permute-start | bytes 1572872 | tf_op jit(solution)/shard_map/ppermute | solution.py:125
  91.6 195.0 %reduce-scatter.2.cloned.1.call-start = ((), (), s32[]{:S(2)}) async-start(), calls=%async_computation.4 | async-start | bytes 5242880 | tf_op jit(solution)/shard_map/reduce_scatter | solution.py:129
  104.8 12.5 %collective-permute-start.6 = (bf16[64,4096]{1,0:T(8,128)(2,1)S(1)}, bf16[64,4096]{1,0:T(8,128)(2,1)}, u32[]{:S(2)}, u32[]{:S(2)}) collective-permute-start(bf16[64,4096]{1,0:T(8,128)(2,1)S(1)} %collective-permute-done.5), channel_id=1, source_target_pairs={{0,1},{1,2},{2,3},{3,4},{4,5},{5,6},{6,7},{7,0},{8,9},{9,10},{10,1... | collective-permute-start | bytes 1572872 | tf_op jit(solution)/shard_map/ppermute | solution.py:125
  117.3 12.2 %collective-permute-start.7 = (bf16[64,4096]{1,0:T(8,128)(2,1)}, bf16[64,4096]{1,0:T(8,128)(2,1)}, u32[]{:S(2)}, u32[]{:S(2)}) collective-permute-start(bf16[64,4096]{1,0:T(8,128)(2,1)} %collective-permute-done.6), channel_id=1, source_target_pairs={{0,1},{1,2},{2,3},{3,4},{4,5},{5,6},{6,7},{7,0},{8,9},{9,10},{10,1... | collective-permute-start | bytes 1572872 | tf_op jit(solution)/shard_map/ppermute | solution.py:125
  151.3 44.9 %copy-start.3 = (f32[512,256]{0,1:T(8,128)}, f32[512,256]{0,1:T(8,128)S(1)}, u32[]{:S(2)}) copy-start(f32[512,256]{0,1:T(8,128)S(1)} %fusion.28) | copy-start | bytes 1572868
  202.1 1.0 copy-start.1
  202.1 1.0 copy-start.2
  203.5 2.3 copy-start.4
  205.8 1.9 copy-start.5
  207.9 6.8 %collective-permute-start = (bf16[512,2,1,128]{3,0,2,1:T(8,128)(2,1)S(1)}, bf16[512,2,1,128]{3,0,2,1:T(8,128)(2,1)S(1)}, u32[]{:S(2)}, u32[]{:S(2)}) collective-permute-start(bf16[512,2,1,128]{3,0,2,1:T(8,128)(2,1)S(1)} %get-tuple-element.431), channel_id=1, source_target_pairs={{0,1},{1,2},{2,3},{3,4},{4,5},{5,6},{6,7},{8,9},{9,10},{10,11},{11... | collective-permute-start | bytes 786440 | tf_op jit(solution)/shard_map/while/body/eval_jaxpr/ppermute | solution.py:15
  218.6 8.3 %collective-permute-start = (bf16[512,2,1,128]{3,0,2,1:T(8,128)(2,1)S(1)}, bf16[512,2,1,128]{3,0,2,1:T(8,128)(2,1)S(1)}, u32[]{:S(2)}, u32[]{:S(2)}) collective-permute-start(bf16[512,2,1,128]{3,0,2,1:T(8,128)(2,1)S(1)} %get-tuple-element.431), channel_id=1, source_target_pairs={{0,1},{1,2},{2,3},{3,4},{4,5},{5,6},{6,7},{8,9},{9,10},{10,11},{11... | collective-permute-start | bytes 786440 | tf_op jit(solution)/shard_map/while/body/eval_jaxpr/ppermute | solution.py:15
Sparse Core Ops, SparseCore 0:
  9.5 73.8 all-gather.5
  84.9 36.3 all-gather.3
  123.4 72.8 all-gather.7
  238.0 48.6 reduce-scatter.1
